TPU v7x, 32 devices: a 4x4x1 block of a 4x4x8 slice. The times are simulated.
32 devices in a mesh: dp: 1 (over z), ff: 4 (over y), hd: 8 (over x, core).
Axes of the slice: x: 4, y: 4, z: 1, core: 2. Of those that a mesh axis runs over, the one named last changes fastest.
The devices are a block of a 4x4x8 slice.
Arguments:
- x_in: bfloat16 [512, 4096], P('dp', 'hd')
- w_up: bfloat16 [4096, 32768], P('hd', 'ff')
- b_up: float32 [32768], P('ff')
- w_down: bfloat16 [16384, 4096], P('ff', 'hd')
- b_down: float32 [4096], P('hd')
- ln_gain: float32 [4096], P('hd')
- ln_bias: float32 [4096], P('hd')
- dy_in: bfloat16 [512, 4096], P('dp', 'hd')
Outputs:
- output 1: bfloat16 [512, 4096], P('dp', 'hd')
- output 2: bfloat16 [512, 4096], P('dp', 'hd')
- output 3: float32 [4096, 32768], P(('dp', 'hd'), 'ff')
- output 4: float32 [16384, 4096], P(('dp', 'ff'), 'hd')
- output 5: float32 [32768], P(('dp', 'ff'))
- output 6: float32 [4096], P(('dp', 'hd'))
- output 7: float32 [4096], P(('dp', 'hd'))
- output 8: float32 [4096], P(('dp', 'hd'))
All inputs are finite; a program needn't handle non-finite values.
Results may differ from a plain program's by a relative error of at most 0.02.
Values are sent between devices in bfloat16 or wider.
A program may use at most 768 MiB of HBM per device.

v0:
```python
import math
import jax
import jax.numpy as jnp
from jax import lax
from jax.sharding import PartitionSpec as P

PAIR = 128
ALPHA = math.sqrt(140.0)
LN_EPS = 1e-5


def gelu_tanh(z_val):
    return jax.nn.gelu(z_val, approximate=True)


def solution(mesh):
    hd_size = mesh.shape['hd']
    data_spec = P('dp', 'hd')
    hid_spec = P('hd')
    in_specs = (data_spec, P('hd', 'ff'), P('ff'), P('ff', 'hd'), hid_spec, hid_spec, hid_spec, data_spec)
    out_specs = (data_spec, data_spec, P(('dp', 'hd'), 'ff'), P(('dp', 'ff'), 'hd'), P(('dp', 'ff')), P(('dp', 'hd')), P(('dp', 'hd')), P(('dp', 'hd')))

    def device_step(x_loc, w_up, b_up, w_down, b_down, ln_gain, ln_bias, dy_loc):
        tokens, hid_loc = x_loc.shape
        hidden = hid_loc * hd_size
        n_blocks = w_up.shape[1] // (2 * PAIR)
        ffn_loc = n_blocks * PAIR
        w_up4 = w_up.reshape(hid_loc, n_blocks, 2, PAIR)
        u_part = jnp.einsum('th,hbkc->tbkc', x_loc, w_up4, preferred_element_type=jnp.float32)
        u_summed = lax.psum(u_part.astype(jnp.bfloat16), 'hd')
        u_act = (u_summed.astype(jnp.float32) + b_up.reshape(n_blocks, 2, PAIR)).astype(jnp.bfloat16)
        val_half = u_act[:, :, 0, :].astype(jnp.float32)
        gate_half = u_act[:, :, 1, :].astype(jnp.float32)
        gelu_out, gelu_vjp = jax.vjp(gelu_tanh, gate_half)
        m_act = (val_half * gelu_out).astype(jnp.bfloat16).reshape(tokens, ffn_loc)
        f_part = jnp.dot(m_act, w_down, preferred_element_type=jnp.float32)
        f_out = lax.psum(f_part.astype(jnp.bfloat16), 'ff').astype(jnp.float32)
        residual = ALPHA * x_loc.astype(jnp.float32) + f_out + b_down
        moments = lax.psum(jnp.stack([jnp.sum(residual, axis=1), jnp.sum(residual * residual, axis=1)]), 'hd')
        row_mean = (moments[0] / hidden)[:, None]
        inv_std = lax.rsqrt(moments[1][:, None] / hidden - row_mean * row_mean + LN_EPS)
        normed = (residual - row_mean) * inv_std
        y_loc = (ln_gain * normed + ln_bias).astype(jnp.bfloat16)
        dy_f = dy_loc.astype(jnp.float32)
        g_dy = dy_f * ln_gain
        grad_moments = lax.psum(jnp.stack([jnp.sum(g_dy, axis=1), jnp.sum(g_dy * normed, axis=1)]), 'hd')
        d_resid = inv_std * (g_dy - (grad_moments[0] / hidden)[:, None] - normed * (grad_moments[1] / hidden)[:, None])
        dr_b = d_resid.astype(jnp.bfloat16)
        dm_part = jnp.einsum('th,fh->tf', dr_b, w_down, preferred_element_type=jnp.float32)
        d_mact = lax.psum(dm_part.astype(jnp.bfloat16), 'hd').astype(jnp.float32).reshape(tokens, n_blocks, PAIR)
        dw_down = jnp.einsum('tf,th->fh', m_act, dr_b, preferred_element_type=jnp.float32)
        d_val = d_mact * gelu_out
        d_gate = gelu_vjp(d_mact * val_half)[0]
        du_f = jnp.stack([d_val, d_gate], axis=2)
        du_b = du_f.astype(jnp.bfloat16)
        dw_up = jnp.einsum('th,tbkc->hbkc', x_loc, du_b, preferred_element_type=jnp.float32).reshape(hid_loc, 2 * ffn_loc)
        dx_part = jnp.einsum('tbkc,hbkc->th', du_b, w_up4, preferred_element_type=jnp.float32)
        dx_sum = lax.psum(dx_part.astype(jnp.bfloat16), 'ff').astype(jnp.float32)
        dx_loc = (ALPHA * d_resid + dx_sum).astype(jnp.bfloat16)
        db_up = jnp.sum(du_f, axis=0).reshape(2 * ffn_loc)
        return (y_loc, dx_loc, dw_up, dw_down, db_up, jnp.sum(d_resid, axis=0), jnp.sum(dy_f * normed, axis=0), jnp.sum(dy_f, axis=0))

    return jax.shard_map(device_step, mesh=mesh, in_specs=in_specs, out_specs=out_specs, check_vma=False)
```

profile of v0, /device:TPU:96, one launch (start us, length us, event | category | flops | bytes accessed | tf_op | source)
XLA Modules:
  0.0 430.7 jit_solution(5312461005674933770)
XLA Ops:
  7.2 0.1 all-reduce.5.cloned.1.call-start
  7.3 14.3 %reshape.85 = bf16[512,32,2,128]{3,2,1,0:T(2,128)(2,1)} reshape(bf16[512,8192]{1,0:T(8,128)(2,1)} %param.9) | data formatting | bytes 16777216 | tf_op jit(solution)/shard_map/reshape | solution.py:28
  21.6 17.2 %fusion.22 = bf16[512,32,2,128]{3,0,2,1:T(8,128)(2,1)} fusion(bf16[512,32,2,128]{3,2,1,0:T(2,128)(2,1)} %reshape.85, bf16[512,512]{1,0:T(8,128)(2,1)S(1)} %copy-done.1), kind=kOutput, calls=%fused_computation.32 | convolution fusion | flops 4299161600 | bytes 17301504 | tf_op jit(solution)/shard_map/th,hbkc->tbkc/dot_general | solution.py:29
  38.8 0.1 all-reduce.5.cloned.1.call-update
  38.9 0.2 all-reduce.7.cloned.1.call-start
  39.1 101.3 %all-reduce.5.cloned.1.call-done = bf16[512,32,2,128]{3,0,2,1:T(8,128)(2,1)} async-done(((bf16[512,32,2,128]{3,0,2,1:T(8,128)(2,1)}), bf16[512,32,2,128]{3,0,2,1:T(8,128)(2,1)}) %all-reduce.5.cloned.1.call-update) | async-done | bytes 8388624 | tf_op jit(solution)/shard_map/psum | solution.py:30
  140.4 9.8 %add_convert_fusion = bf16[512,32,2,128]{3,0,2,1:T(8,128)(2,1)} fusion(bf16[512,32,2,128]{3,0,2,1:T(8,128)(2,1)} %all-reduce.5.cloned.1.call-done, f32[32,2,128]{2,1,0:T(2,128)S(1)} %bitcast.37), kind=kLoop, calls=%fused_computation.1 | loop fusion | flops 12582912 | bytes 16809984 | tf_op jit(solution)/shard_map/convert_element_type | solution.py:31
  150.2 11.6 %slice_convert_fusion = (f32[512,32,1,128]{3,0,2,1:T(8,128)}, f32[512,32,1,128]{3,0,2,1:T(8,128)}) fusion(bf16[512,32,2,128]{3,0,2,1:T(8,128)(2,1)} %add_convert_fusion), kind=kLoop, calls=%fused_computation.34 | loop fusion | flops 4194304 | bytes 25165824 | tf_op jit(solution)/shard_map/convert_element_type | solution.py:32
  161.9 9.0 %copy.21 = f32[512,32,1,128]{0,3,1,2:T(8,128)} copy(f32[512,32,1,128]{3,0,2,1:T(8,128)} %get-tuple-element.34) | data formatting | bytes 16777216 | tf_op jit(solution)/shard_map/convert_element_type | solution.py:32
  170.9 8.9 %copy.22 = f32[512,32,1,128]{0,3,1,2:T(8,128)} copy(f32[512,32,1,128]{3,0,2,1:T(8,128)} %get-tuple-element.35) | data formatting | bytes 16777216 | tf_op jit(solution)/shard_map/convert_element_type | solution.py:33
  179.9 7.4 %fusion.17 = bf16[512,4096]{0,1:T(8,128)(2,1)S(1)} fusion(f32[512,32,1,128]{0,3,1,2:T(8,128)} %copy.22, f32[512,32,1,128]{0,3,1,2:T(8,128)} %copy.21), kind=kLoop, calls=%fused_computation.27 | loop fusion | flops 20971520 | bytes 20971520 | tf_op jit(solution)/shard_map/convert_element_type | solution.py:35
  187.3 2.0 copy-done
  189.3 3.1 convolution_convert_fusion.1
  192.5 0.1 all-reduce.9.cloned.1.call-start
  192.6 37.7 %all-reduce.7.cloned.1.call-done = bf16[512,512]{1,0:T(8,128)(2,1)} async-done(((bf16[512,512]{1,0:T(8,128)(2,1)}), bf16[512,512]{1,0:T(8,128)(2,1)}) %all-reduce.7.cloned.1.call-update) | async-done | bytes 524304 | tf_op jit(solution)/shard_map/psum | solution.py:37
  230.3 1.4 fusion.41
  231.7 12.5 %psum.44 = f32[2,512]{1,0:T(2,128)S(1)} all-reduce(f32[2,512]{1,0:T(2,128)S(1)} %pad_maximum_fusion.1), channel_id=1, replica_groups=mesh['dp'=1,'ff'=4,'hd'=8] {'hd'}, use_global_device_ids=true, to_apply=%region_4.0 | all-reduce | flops 1024 | bytes 8192 | tf_op jit(solution)/shard_map/psum | solution.py:39
  244.3 2.3 fusion.40
  246.6 12.5 %psum.45 = f32[2,512]{1,0:T(2,128)S(1)} all-reduce(f32[2,512]{1,0:T(2,128)S(1)} %pad_maximum_fusion.2), channel_id=1, replica_groups=mesh['dp'=1,'ff'=4,'hd'=8] {'hd'}, use_global_device_ids=true, to_apply=%region_7.0 | all-reduce | flops 1024 | bytes 8192 | tf_op jit(solution)/shard_map/psum | solution.py:46
  259.1 3.0 fusion.49
  262.1 6.6 %convolution_convert_fusion = bf16[512,4096]{1,0:T(8,128)(2,1)} fusion(bf16[4096,512]{1,0:T(8,128)(2,1)} %param.11, f32[512,512]{1,0:T(8,128)S(1)} %get-tuple-element.31), kind=kOutput, calls=%fused_computation.33 | convolution fusion | flops 2149842944 | bytes 9437184 | tf_op jit(solution)/shard_map/th,fh->tf/dot_general | solution.py:49
  268.7 6.5 %copy.23 = bf16[512,4096]{0,1:T(8,128)(2,1)} copy(bf16[512,4096]{1,0:T(8,128)(2,1)} %convolution_convert_fusion) | data formatting | bytes 8388608 | tf_op jit(solution)/shard_map/convert_element_type | solution.py:50
  275.1 6.4 %copy.24 = bf16[512,32,1,128]{3,0,2,1:T(8,128)(2,1)} copy(bf16[512,32,1,128]{0,3,1,2:T(8,128)(2,1)} %bitcast.36) | data formatting | bytes 8388608 | tf_op jit(solution)/shard_map/reshape | solution.py:50
  281.6 0.3 all-reduce.11.cloned.1.call-start
  281.9 7.9 %fusion.44 = f32[4096,512]{1,0:T(8,128)} fusion(bf16[512,4096]{0,1:T(8,128)(2,1)} %copy-done, f32[512,512]{1,0:T(8,128)S(1)} %get-tuple-element.31), kind=kOutput, calls=%fused_computation.58 | convolution fusion | flops 2147745792 | bytes 13631488 | tf_op jit(solution)/shard_map/tf,th->fh/dot_general | solution.py:51
  289.8 57.3 %all-reduce.9.cloned.1.call-done = bf16[512,32,1,128]{3,0,2,1:T(8,128)(2,1)} async-done(((bf16[512,32,1,128]{3,0,2,1:T(8,128)(2,1)}), bf16[512,32,1,128]{3,0,2,1:T(8,128)(2,1)}) %all-reduce.9.cloned.1.call-update) | async-done | bytes 4194320 | tf_op jit(solution)/shard_map/psum | solution.py:50
  347.2 13.1 %convert_multiply_fusion.1 = (f32[512,32,1,128]{3,0,2,1:T(8,128)}, f32[512,32,1,128]{3,0,2,1:T(8,128)}) fusion(bf16[512,32,1,128]{3,0,2,1:T(8,128)(2,1)} %all-reduce.9.cloned.1.call-done, bf16[512,32,2,128]{3,0,2,1:T(8,128)(2,1)} %add_convert_fusion), kind=kLoop, calls=%fused_computation.8 | loop fusion | flops 52428800 | bytes 29360128 | tf_op jit(solution)/shard_map/mul | solution.py:52
  360.3 19.5 %fusion.31 = bf16[512,512]{1,0:T(8,128)(2,1)} fusion(bf16[512,32,2,128]{3,2,1,0:T(2,128)(2,1)} %reshape.85, f32[512,32,1,128]{3,0,2,1:T(8,128)} %get-tuple-element.33, f32[512,32,1,128]{3,0,2,1:T(8,128)} %get-tuple-element.32), kind=kOutput, calls=%fused_computation.43 | convolution fusion | flops 4299423744 | bytes 25690112 | tf_op jit(solution)/shard_map/tbkc,hbkc->th/dot_general | solution.py:57
  379.8 16.3 %fusion.34 = f32[32,2,128,512]{3,2,1,0:T(8,128)} fusion(f32[512,32,1,128]{3,0,2,1:T(8,128)} %get-tuple-element.33, f32[512,32,1,128]{3,0,2,1:T(8,128)} %get-tuple-element.32, bf16[512,512]{1,0:T(8,128)(2,1)S(1)} %copy-done.1), kind=kOutput, calls=%fused_computation.45 | convolution fusion | flops 4299161600 | bytes 34078720 | tf_op jit(solution)/shard_map/th,tbkc->hbkc/dot_general | solution.py:56
  396.2 17.4 %copy.27 = f32[512,8192]{1,0:T(8,128)} copy(f32[512,8192]{0,1:T(8,128)} %bitcast.35) | data formatting | bytes 33554432
  413.6 8.1 %fusion = f32[32,2,128]{2,1,0:T(2,128)} fusion(f32[512,32,1,128]{3,0,2,1:T(8,128)} %get-tuple-element.33, f32[512,32,1,128]{3,0,2,1:T(8,128)} %get-tuple-element.32), kind=kLoop, calls=%fused_computation.2 | loop fusion | flops 8380416 | bytes 16809984 | tf_op jit(solution)/shard_map/reduce_sum | solution.py:60
  421.7 2.0 add_convert_fusion.1
  (24 shorter events, 0.2 us)
Async XLA Ops:
  7.2 14.4 %copy-start.1 = (bf16[512,512]{1,0:T(8,128)(2,1)S(1)}, bf16[512,512]{1,0:T(8,128)(2,1)}, u32[]{:S(2)}) copy-start(bf16[512,512]{1,0:T(8,128)(2,1)} %param.8) | copy-start | bytes 1572868
  7.2 133.2 %all-reduce.5.cloned.1.call-start = ((), (), s32[]{:S(2)}) async-start(), calls=%async_computation | async-start | bytes 16777216 | tf_op jit(solution)/shard_map/psum | solution.py:30
  38.8 101.6 %copy-start.3 = (f32[8192]{0:T(1024)S(1)}, f32[8192]{0:T(1024)}, u32[]{:S(2)}) copy-start(f32[8192]{0:T(1024)} %param.10) | copy-start | bytes 98308
  38.9 191.4 %all-reduce.7.cloned.1.call-start = ((), (), s32[]{:S(2)}) async-start(), calls=%async_computation.1 | async-start | bytes 1048576 | tf_op jit(solution)/shard_map/psum | solution.py:37
  179.9 9.4 %copy-start.7 = (bf16[4096,512]{1,0:T(8,128)(2,1)S(1)}, bf16[4096,512]{1,0:T(8,128)(2,1)}, u32[]{:S(2)}) copy-start(bf16[4096,512]{1,0:T(8,128)(2,1)} %param.11) | copy-start | bytes 12582916
  187.3 2.0 copy-start
  189.3 41.0 %copy-start.4 = (f32[512]{0:T(512)S(1)}, f32[512]{0:T(512)}, u32[]{:S(2)}) copy-start(f32[512]{0:T(512)} %param.12) | copy-start | bytes 6148
  189.3 55.0 %copy-start.2 = (bf16[512,512]{1,0:T(8,128)(2,1)S(1)}, bf16[512,512]{1,0:T(8,128)(2,1)}, u32[]{:S(2)}) copy-start(bf16[512,512]{1,0:T(8,128)(2,1)} %param.15) | copy-start | bytes 1572868
  189.3 55.0 %copy-start.5 = (f32[512]{0:T(512)S(1)}, f32[512]{0:T(512)}, u32[]{:S(2)}) copy-start(f32[512]{0:T(512)} %param.13) | copy-start | bytes 6148
  189.3 69.8 %copy-start.6 = (f32[512]{0:T(512)S(1)}, f32[512]{0:T(512)}, u32[]{:S(2)}) copy-start(f32[512]{0:T(512)} %param.14) | copy-start | bytes 6148
  192.5 154.7 %all-reduce.9.cloned.1.call-start = ((), (), s32[]{:S(2)}) async-start(), calls=%async_computation.2 | async-start | bytes 8388608 | tf_op jit(solution)/shard_map/psum | solution.py:50
  281.6 140.1 %all-reduce.11.cloned.1.call-start = ((), (), s32[]{:S(2)}) async-start(), calls=%async_computation.3 | async-start | bytes 1048576 | tf_op jit(solution)/shard_map/psum | solution.py:58
Sparse Core Ops, SparseCore 0:
  39.0 101.3 all-reduce.4
  192.6 37.6 all-reduce.6
  281.7 65.3 all-reduce.8
  380.0 37.6 all-reduce.10
where the time goes:
time: 437 us; the launch traced here: 431 us
  waiting for transfers between devices  197 us (45%)
  matrix products  70.7 us (16%)
  local copies, waits for them, and re-layouts  64.6 us (15%)
  other arithmetic  58.9 us (13%)
  blocking collectives  25 us (6%)
  between operations  14.3 us (3%)
    psum x1, waiting for transfers between devices, device_step(): u_summed = lax.psum(u_part.astype(jnp.bfloat16), 'hd')  101 us
    psum x1, waiting for transfers between devices, device_step(): lax.psum(dm_part.astype(jnp.bfloat16), 'hd').astype(jnp.float32)  57.3 us
    psum x1, waiting for transfers between devices, device_step(): f_out = lax.psum(f_part.astype(jnp.bfloat16), 'ff').astype(jnp.float32)  37.7 us
    dot_general x1, matrix products, device_step(): jnp.einsum('tbkc,hbkc->th', du_b, w_up4, preferred_element_type=jnp.float32)  19.5 us
    unnamed x17, local copies, waits for them, and re-layouts  19.4 us
    dot_general x1, matrix products, device_step(): jnp.einsum('th,hbkc->tbkc', x_loc, w_up4, preferred_element_type=jnp.floa...  17.2 us
    dot_general x1, matrix products, device_step(): jnp.einsum('th,tbkc->hbkc', x_loc, du_b, preferred_element_type=jnp.float32)  16.3 us
    reshape x1, local copies, waits for them, and re-layouts, device_step(): w_up4 = w_up.reshape(hid_loc, n_blocks, 2, PAIR)  14.3 us
  transfers between devices with their start and end apart: 4, of which 3 were waited for; matrix products, arithmetic and copies ran while one was open for 12% of the time, Pallas kernels for 0%

commit v1 on v0

v1 whole, which is shorter than its diff:
```python
import functools
import math
import jax
import jax.numpy as jnp
from jax import lax
from jax.experimental import pallas as pl
from jax.experimental.pallas import tpu as pltpu
from jax.sharding import PartitionSpec as P

PAIR = 128
ALPHA = math.sqrt(140.0)
LN_EPS = 1e-5
CORES = 2
NCHUNK = 2
F32 = jnp.float32
BF16 = jnp.bfloat16
MESH = pl.DeviceIdType.MESH
GELU_C = math.sqrt(2.0 / math.pi)
GELU_A = 0.044715


def dot_nn(a, b):
    return lax.dot_general(a, b, (((1,), (0,)), ((), ())), preferred_element_type=F32)


def dot_nt(a, b):
    return lax.dot_general(a, b, (((1,), (1,)), ((), ())), preferred_element_type=F32)


def dot_tn(a, b):
    return lax.dot_general(a, b, (((0,), (0,)), ((), ())), preferred_element_type=F32)


def mlp_kernel(cfg, x_hbm, w1_hbm, b1_ref, w2_hbm, b2_ref, gam_ref, bet_ref, dy_hbm,
               y_out, d_out, m_out, du_out, dxp_out, drq_out, db1_out, small_out,
               xo, xx, dyv, w1v, w1x, w2v, w2x,
               ps1, rf1, rn1, own1, ps2, rf2, rn2, own2, uo, mb, dub,
               facc, fs, fr, rbuf, drq, st, do, dx, yv, dbuf, cs, csr, dxacc, dxs,
               s_sem, r_sem, l_sem):
    nff, nhd, T, HL, UH, FB = cfg
    nx = nhd // CORES
    FH = FB // 2
    TC = T // NCHUNK
    TQ = TC // nff
    hidden = HL * nhd
    h_me = lax.axis_index("hd")
    y_me = lax.axis_index("ff")
    x_me = lax.div(h_me, CORES)
    c_me = lax.rem(h_me, CORES)
    c_ot = 1 - c_me

    def xdev(off):
        return {"hd": lax.rem(x_me + off, nx) * CORES + c_me}

    XP, XM = xdev(1), xdev(nx - 1)
    CO = {"hd": x_me * CORES + c_ot}

    def ydev(s):
        return {"ff": lax.rem(y_me + s, nff)}

    def hdev(s):
        return {"hd": lax.rem(h_me + s, nhd)}

    def quarter(off):
        return lax.rem(x_me + off, nx)

    def block(off):
        return c_me * nx + quarter(off)

    b_own = block(0)

    bar = pltpu.get_barrier_semaphore()
    for s in range(1, nhd):
        pl.semaphore_signal(bar, inc=1, device_id=hdev(s), device_id_type=MESH)
    for s in range(1, nff):
        pl.semaphore_signal(bar, inc=1, device_id=ydev(s), device_id_type=MESH)

    cnt = {"r": 0, "l": 0}
    sent = []
    D = {}

    def rsend(name, src, dst, dev):
        i = cnt["r"]
        cnt["r"] += 1
        cp = pltpu.make_async_remote_copy(src_ref=src, dst_ref=dst, send_sem=s_sem.at[i], recv_sem=r_sem.at[i],
                                          device_id=dev, device_id_type=MESH)
        cp.start()
        sent.append(cp)
        D[name] = cp

    def rwait(name):
        D[name].wait_recv()

    def lcopy(name, src, dst):
        i = cnt["l"]
        cnt["l"] += 1
        cp = pltpu.make_async_copy(src, dst, l_sem.at[i])
        cp.start()
        D[name] = cp

    def lwait(name):
        D[name].wait()

    order = (2, 1, nx - 1, 0)
    lcopy("x", x_hbm, xo)

    def load_half(b, h):
        return w1_hbm.at[:, pl.ds(pl.multiple_of((2 * b + h) * UH, UH), UH)]

    for j, off in enumerate(order):
        for h in range(2):
            lcopy(("w1", j, h), load_half(block(off), h), w1v.at[2 * block(off) + h])
    lcopy("dy", dy_hbm, dyv)
    lcopy("w2", w2_hbm, w2v)
    pl.semaphore_wait(bar, nhd - 1 + nff - 1)
    rsend("xx", x_hbm, xx, CO)
    for j, off in enumerate(order):
        for h in range(2):
            q = quarter(off)
            rsend(("w1x", j, h), load_half(c_ot * nx + q, h), w1x.at[2 * q + h], CO)
    rsend("w2x", w2_hbm.at[pl.ds(c_ot * nx, nx)], w2x, CO)
    for q in range(nx):
        for h in range(2):
            b = c_ot * nx + q
            lcopy(("w1o", q, h), load_half(b, h), w1v.at[2 * b + h])

    def rows(k):
        return pl.ds(k * TC, TC)

    def rs_first(tag, k, j, ps, rf, rn):
        if j == 0:
            rsend((tag, "fA", k), ps.at[0, 0, rows(k)], rf.at[0, rows(k)], XP)
            rsend((tag, "fB", k), ps.at[0, 1, rows(k)], rf.at[1, rows(k)], XM)
        elif j == 1:
            rsend((tag, "nB", k), ps.at[1, 1, rows(k)], rn.at[0, 1, rows(k)], XP)
        elif j == 2:
            rsend((tag, "nA", k), ps.at[2, 0, rows(k)], rn.at[1, 0, rows(k)], XM)

    def rs_combine(tag, k, ps, rf, rn):
        for d, (nm, out, j, h, dev) in enumerate((("fA", "cA", 1, 0, XP), ("fB", "cB", 2, 1, XM))):
            rwait((tag, nm, k))
            ps[j, h, rows(k)] = (ps[j, h, rows(k)].astype(F32) + rf[d, rows(k)].astype(F32)).astype(BF16)
            rsend((tag, out, k), ps.at[j, h, rows(k)], rn.at[d, h, rows(k)], dev)

    def rs_wait(tag, k):
        for nm in ("nB", "nA", "cA", "cB"):
            rwait((tag, nm, k))

    def ag_first(tag, k, view):
        for nm, dev in (("p", XP), ("m", XM), ("o0", CO)):
            rsend((tag, nm, k), view(b_own, rows(k)), view(b_own, rows(k)), dev)

    def ag_forward(tag, k, view):
        half = TC // 2
        ra, rb = pl.ds(k * TC, half), pl.ds(k * TC + half, half)
        bm, bp = block(nx - 1), block(1)
        rwait((tag, "p", k))
        rsend((tag, "fA", k), view(bm, ra), view(bm, ra), XP)
        rsend((tag, "o1", k), view(bm, rows(k)), view(bm, rows(k)), CO)
        rwait((tag, "m", k))
        rsend((tag, "fB", k), view(bp, rb), view(bp, rb), XM)
        rsend((tag, "o2", k), view(bp, rows(k)), view(bp, rows(k)), CO)

    def ag_last(tag, k, view):
        bf = block(2)
        rwait((tag, "fA", k))
        rwait((tag, "fB", k))
        rsend((tag, "o3", k), view(bf, rows(k)), view(bf, rows(k)), CO)
        for i in range(4):
            rwait((tag, "o%d" % i, k))

    def m_view(b, r):
        return mb.at[b, r]

    def du_view(b, r):
        return dub.at[pl.ds(2 * b, 2), r]

    def u_partial(k):
        for j, off in enumerate(order):
            for h in range(2):
                if k == 0:
                    lwait(("w1", j, h))
                    rwait(("w1x", j, h))
            b, q = block(off), quarter(off)

            @pl.loop(0, 2)
            def _(h):
                p = dot_nn(xo[rows(k)], w1v[2 * b + h]) + dot_nn(xx[rows(k)], w1x[2 * q + h])
                if j < 3:
                    ps1[j, h, rows(k)] = p.astype(BF16)
                else:
                    own1[h, rows(k)] = p

            if k == 0:
                rs_first("U", k, j, ps1, rf1, rn1)

    def u_send(k):
        for j in range(3):
            rs_first("U", k, j, ps1, rf1, rn1)

    TS = 32

    def activate(k):
        rs_wait("U", k)
        bias = b1_ref[pl.ds(b_own, 1), :]

        @pl.loop(0, TC // TS)
        def _(i):
            r = pl.ds(pl.multiple_of(k * TC + i * TS, TS), TS)
            for h in range(2):
                u = own1[h, r] + rn1[0, h, r].astype(F32) + rn1[1, h, r].astype(F32)
                u = (u + bias[:, h * UH:(h + 1) * UH]).astype(BF16)
                uo[h, r] = u
                for p in range(UH // (2 * PAIR)):
                    v = u[:, 2 * p * PAIR:(2 * p + 1) * PAIR].astype(F32)
                    g = u[:, (2 * p + 1) * PAIR:(2 * p + 2) * PAIR].astype(F32)
                    t = jnp.tanh(GELU_C * (g + GELU_A * (g * g * g)))
                    m = v * (g * (0.5 * (1.0 + t)))
                    lo = h * FH + p * PAIR
                    mb[b_own, r, lo:lo + PAIR] = m.astype(BF16)

        ag_first("M", k, m_view)

    def f_partial(k):
        ag_last("M", k, m_view)
        lcopy(("mo", k), mb.at[:, rows(k)], m_out.at[:, rows(k)])
        facc[k] = jnp.zeros_like(facc[k])
        if k == 0:
            lwait("w2")

        @pl.loop(0, nhd)
        def _(b):
            facc[k] += dot_nn(mb[b, rows(k)], w2v[b])

        fs[rows(k)] = facc[k].astype(BF16)
        for s in range(1, nff):
            yy = lax.rem(y_me + s, nff)
            rsend(("f", s, k), fs.at[pl.ds(pl.multiple_of(k * TC + yy * TQ, TQ), TQ)], fr.at[k, s - 1], ydev(s))

    def q_rows(k, yy):
        return pl.ds(pl.multiple_of(k * TC + yy * TQ, TQ), TQ)

    def ln_stats(k):
        if k == 0:
            lwait("dy")
        for s in range(1, nff):
            rwait(("f", s, k))
        r = facc[k, pl.ds(pl.multiple_of(y_me * TQ, TQ), TQ)]
        for s in range(1, nff):
            r = r + fr[k, s - 1].astype(F32)
        r = ALPHA * xo[q_rows(k, y_me)].astype(F32) + r + b2_ref[0:1, :]
        rbuf[k] = r
        g = dyv[q_rows(k, y_me)].astype(F32) * gam_ref[0:1, :]
        mean = jnp.sum(r, axis=1, keepdims=True) * (1.0 / HL)
        rc = r - mean
        m2 = jnp.sum(rc * rc, axis=1, keepdims=True)
        gs = jnp.sum(g, axis=1, keepdims=True)
        gc = jnp.sum(g * rc, axis=1, keepdims=True)
        lane = lax.broadcasted_iota(jnp.int32, (TQ, 128), 1)
        cols = jnp.where(lane == 0, mean, jnp.where(lane == 1, m2, jnp.where(lane == 2, gs, jnp.where(lane == 3, gc, 0.0))))
        full = jnp.concatenate([cols, jnp.zeros((128 - TQ, 128), F32)], axis=0) if TQ < 128 else cols
        st[k, h_me] = full.T[0:8, :]
        for s in range(1, nhd):
            rsend(("st", s, k), st.at[k, h_me], st.at[k, h_me], hdev(s))

    def ln_apply(k):
        for s in range(1, nhd):
            rwait(("st", s, k))
        mean_sum = jnp.zeros((1, 128), F32)
        for i in range(nhd):
            mean_sum = mean_sum + st[k, i, 0:1, :]
        mu = mean_sum * (1.0 / nhd)
        ss = jnp.zeros((1, 128), F32)
        gs = jnp.zeros((1, 128), F32)
        gr = jnp.zeros((1, 128), F32)
        for i in range(nhd):
            dev = st[k, i, 0:1, :] - mu
            ss = ss + st[k, i, 1:2, :] + HL * (dev * dev)
            gs = gs + st[k, i, 2:3, :]
            gr = gr + st[k, i, 3:4, :] + dev * st[k, i, 2:3, :]
        rho = lax.rsqrt(ss * (1.0 / hidden) + LN_EPS)
        gm = gs * (1.0 / hidden)
        grm = rho * gr * (1.0 / hidden)
        row = lax.broadcasted_iota(jnp.int32, (128, 128), 0)
        z = jnp.where(row == 0, mu, jnp.where(row == 1, rho, jnp.where(row == 2, gm, jnp.where(row == 3, grm, 0.0))))
        z = z.T[0:TQ, :]
        mu, rho, gm, grm = z[:, 0:1], z[:, 1:2], z[:, 2:3], z[:, 3:4]
        normed = (rbuf[k] - mu) * rho
        qr = q_rows(k, y_me)
        dyq = dyv[qr].astype(F32)
        g = dyq * gam_ref[0:1, :]
        dr = rho * (g - gm - normed * grm)
        drq[k] = dr
        do[qr] = dr.astype(BF16)
        for s in range(1, nff):
            rsend(("d", s, k), do.at[qr], do.at[qr], ydev(s))
        rsend(("dc", 0, k), do.at[qr], dx.at[qr], CO)
        yv[qr] = (gam_ref[0:1, :] * normed + bet_ref[0:1, :]).astype(BF16)
        for s in range(1, nff):
            rsend(("y", s, k), yv.at[qr], yv.at[qr], ydev(s))
        cs[0:1, :] += jnp.sum(dr, axis=0, keepdims=True)
        cs[1:2, :] += jnp.sum(dyq * normed, axis=0, keepdims=True)

    def d_forward(k):
        for s in range(1, nff):
            rwait(("d", s, k))
            qr = q_rows(k, lax.rem(y_me + nff - s, nff))
            rsend(("dc", s, k), do.at[qr], dx.at[qr], CO)

    def dm_partial(k):
        if k == 0:
            rwait("w2x")
        for s in range(nff):
            rwait(("dc", s, k))
        for j, off in enumerate(order):
            b, q = block(off), quarter(off)
            p = dot_nt(do[rows(k)], w2v[b]) + dot_nt(dx[rows(k)], w2x[q])
            for h in range(2):
                ph = p[:, h * FH:(h + 1) * FH]
                if j < 3:
                    ps2[j, h, rows(k)] = ph.astype(BF16)
                else:
                    own2[h, rows(k)] = ph
            rs_first("G", k, j, ps2, rf2, rn2)

    def du_make(k):
        rs_wait("G", k)

        @pl.loop(0, TC // TS)
        def _(i):
            r = pl.ds(pl.multiple_of(k * TC + i * TS, TS), TS)
            for h in range(2):
                dm = own2[h, r] + rn2[0, h, r].astype(F32) + rn2[1, h, r].astype(F32)
                u = uo[h, r]
                for p in range(UH // (2 * PAIR)):
                    v = u[:, 2 * p * PAIR:(2 * p + 1) * PAIR].astype(F32)
                    g = u[:, (2 * p + 1) * PAIR:(2 * p + 2) * PAIR].astype(F32)
                    dmp = dm[:, p * PAIR:(p + 1) * PAIR]
                    gg = g * g
                    t = jnp.tanh(GELU_C * (g + GELU_A * (gg * g)))
                    cdf = 0.5 * (1.0 + t)
                    dv = dmp * (g * cdf)
                    slope = cdf + (0.5 * g) * (1.0 - t * t) * (GELU_C * (1.0 + 3.0 * GELU_A * gg))
                    dg = dmp * v * slope
                    lo = 2 * p * PAIR
                    dub[2 * b_own + h, r, lo:lo + PAIR] = dv.astype(BF16)
                    dub[2 * b_own + h, r, lo + PAIR:lo + 2 * PAIR] = dg.astype(BF16)
                    sl = h * (UH // PAIR) + 2 * p
                    dbuf[b_own, sl:sl + 1, :] += jnp.sum(dv, axis=0, keepdims=True)
                    dbuf[b_own, sl + 1:sl + 2, :] += jnp.sum(dg, axis=0, keepdims=True)

        ag_first("V", k, du_view)

    def dx_partial(k):
        ag_last("V", k, du_view)
        lcopy(("duo", k), dub.at[:, rows(k)], du_out.at[:, rows(k)])
        dxacc[...] = jnp.zeros_like(dxacc)
        if k == 0:
            for q in range(nx):
                for h in range(2):
                    lwait(("w1o", q, h))

        @pl.loop(0, 2 * nhd)
        def _(i):
            dxacc[...] += dot_nt(dub[i, rows(k)], w1v[i])

        dxs[rows(k)] = dxacc[...].astype(BF16)
        lcopy(("dxo", k), dxs.at[rows(k)], dxp_out.at[rows(k)])

    cs[...] = jnp.zeros_like(cs)
    dbuf[b_own] = jnp.zeros_like(dbuf[b_own])
    lwait("x")
    rwait("xx")
    u_partial(0)
    u_partial(1)
    rs_combine("U", 0, ps1, rf1, rn1)
    u_send(1)
    activate(0)
    rs_combine("U", 1, ps1, rf1, rn1)
    ag_forward("M", 0, m_view)
    activate(1)
    f_partial(0)
    ag_forward("M", 1, m_view)
    ln_stats(0)
    ln_apply(0)
    f_partial(1)
    d_forward(0)
    ln_stats(1)
    dm_partial(0)
    ln_apply(1)
    rs_combine("G", 0, ps2, rf2, rn2)
    for s in range(1, nff):
        rsend(("cs", s), cs, csr.at[s - 1], ydev(s))
    d_forward(1)
    du_make(0)
    dm_partial(1)
    ag_forward("V", 0, du_view)
    rs_combine("G", 1, ps2, rf2, rn2)
    du_make(1)
    for s in range(1, nhd):
        rsend(("db", s), dbuf.at[b_own], dbuf.at[b_own], hdev(s))
    dx_partial(0)
    ag_forward("V", 1, du_view)
    lcopy("do", do, d_out)
    lcopy("dro", drq, drq_out)
    for k in range(NCHUNK):
        for s in range(1, nff):
            rwait(("y", s, k))
    lcopy("yo", yv, y_out)
    tot = cs[...]
    for s in range(1, nff):
        rwait(("cs", s))
        tot = tot + csr[s - 1]
    small_out[0:2, :] = tot[0:2, :]
    small_out[2:3, :] = jnp.sum(dyv[...].astype(F32), axis=0, keepdims=True)
    small_out[3:8, :] = jnp.zeros((5, HL), F32)
    for s in range(1, nhd):
        rwait(("db", s))
    db1_out[...] = dbuf[...]
    dx_partial(1)
    for nm in ("do", "dro", "yo"):
        lwait(nm)
    for k in range(NCHUNK):
        for nm in ("mo", "duo", "dxo"):
            lwait((nm, k))
    for cp in sent:
        cp.wait_send()


def comm_call(mesh, x, w1, b1, w2, b2, gam, bet, dy):
    nff, nhd = mesh.shape['ff'], mesh.shape['hd']
    T, HL = x.shape
    UH = w1.shape[1] // (2 * nhd)
    FB = w2.shape[0] // nhd
    FH = FB // 2
    TC = T // NCHUNK
    TQ = TC // nff
    nx = nhd // CORES
    V = pltpu.VMEM
    scratch = [
        V((T, HL), BF16), V((T, HL), BF16), V((T, HL), BF16),
        V((2 * nhd, HL, UH), BF16), V((2 * nx, HL, UH), BF16), V((nhd, FB, HL), BF16), V((nx, FB, HL), BF16),
        V((3, 2, T, UH), BF16), V((2, T, UH), BF16), V((2, 2, T, UH), BF16), V((2, T, UH), F32),
        V((3, 2, T, FH), BF16), V((2, T, FH), BF16), V((2, 2, T, FH), BF16), V((2, T, FH), F32),
        V((2, T, UH), BF16), V((nhd, T, FB), BF16), V((2 * nhd, T, UH), BF16),
        V((NCHUNK, TC, HL), F32), V((T, HL), BF16), V((NCHUNK, nff - 1, TQ, HL), BF16),
        V((NCHUNK, TQ, HL), F32), V((NCHUNK, TQ, HL), F32), V((NCHUNK, nhd, 8, 128), F32),
        V((T, HL), BF16), V((T, HL), BF16), V((T, HL), BF16),
        V((nhd, 2 * UH // 128, 128), F32), V((8, HL), F32), V((nff - 1, 8, HL), F32),
        V((TC, HL), F32), V((T, HL), BF16),
        pltpu.SemaphoreType.DMA((160,)), pltpu.SemaphoreType.DMA((160,)), pltpu.SemaphoreType.DMA((40,)),
    ]
    anyspec = pl.BlockSpec(memory_space=pl.ANY)
    vspec = pl.BlockSpec(memory_space=pltpu.VMEM)
    S = jax.ShapeDtypeStruct
    return pl.pallas_call(
        functools.partial(mlp_kernel, (nff, nhd, T, HL, UH, FB)),
        out_shape=[S((T, HL), BF16), S((T, HL), BF16), S((nhd, T, FB), BF16), S((2 * nhd, T, UH), BF16),
                   S((T, HL), BF16), S((NCHUNK, TQ, HL), F32), S((nhd, 2 * UH // 128, 128), F32), S((8, HL), F32)],
        in_specs=[anyspec, anyspec, vspec, anyspec, vspec, vspec, vspec, anyspec],
        out_specs=[anyspec, anyspec, anyspec, anyspec, anyspec, anyspec, vspec, vspec],
        scratch_shapes=scratch,
        compiler_params=pltpu.CompilerParams(collective_id=0, has_side_effects=True, vmem_limit_bytes=67043328),
        name="mlp_comm",
    )(x, w1, b1.reshape(nhd, 2 * UH), w2.reshape(nhd, FB, HL), b2.reshape(1, HL), gam.reshape(1, HL), bet.reshape(1, HL), dy)


def dw2_kernel(m_ref, d_ref, o_ref):
    o_ref[...] = dot_tn(m_ref[0], d_ref[...])


def dw1_kernel(x_ref, du_ref, o_ref):
    o_ref[...] = dot_tn(x_ref[...], du_ref[0])


def weight_grads(x, d, m, du):
    n2, T, FB = m.shape
    n1, _, UH = du.shape
    HL = x.shape[1]
    dw2 = pl.pallas_call(
        dw2_kernel, grid=(n2,), out_shape=jax.ShapeDtypeStruct((n2 * FB, HL), F32),
        in_specs=[pl.BlockSpec((1, T, FB), lambda i: (i, 0, 0)), pl.BlockSpec((T, HL), lambda i: (0, 0))],
        out_specs=pl.BlockSpec((FB, HL), lambda i: (i, 0)),
        cost_estimate=pl.CostEstimate(flops=2 * n2 * FB * HL * T, bytes_accessed=n2 * FB * HL * 4 + n2 * FB * T * 2, transcendentals=0),
        name="dw2",
    )(m, d)
    dw1 = pl.pallas_call(
        dw1_kernel, grid=(n1,), out_shape=jax.ShapeDtypeStruct((HL, n1 * UH), F32),
        in_specs=[pl.BlockSpec((T, HL), lambda i: (0, 0)), pl.BlockSpec((1, T, UH), lambda i: (i, 0, 0))],
        out_specs=pl.BlockSpec((HL, UH), lambda i: (0, i)),
        cost_estimate=pl.CostEstimate(flops=2 * n1 * UH * HL * T, bytes_accessed=n1 * UH * HL * 4 + n1 * UH * T * 2, transcendentals=0),
        name="dw1",
    )(x, du)
    return dw1, dw2


def solution(mesh):
    nff = mesh.shape['ff']
    data_spec = P('dp', 'hd')
    hid_spec = P('hd')
    in_specs = (data_spec, P('hd', 'ff'), P('ff'), P('ff', 'hd'), hid_spec, hid_spec, hid_spec, data_spec)
    out_specs = (data_spec, data_spec, P(('dp', 'hd'), 'ff'), P(('dp', 'ff'), 'hd'), P(('dp', 'ff')), P(('dp', 'hd')), P(('dp', 'hd')), P(('dp', 'hd')))

    def shift(v, s):
        return lax.ppermute(v, 'ff', [(i, (i + s) % nff) for i in range(nff)])

    def device_step(x_loc, w_up, b_up, w_down, b_down, ln_gain, ln_bias, dy_loc):
        T, HL = x_loc.shape
        y_loc, d_loc, m_all, du_all, dxp, drq, db1, small = comm_call(
            mesh, x_loc, w_up, b_up, w_down, b_down, ln_gain, ln_bias, dy_loc)
        y_me = lax.axis_index('ff')
        TQ = T // (NCHUNK * nff)
        parts = dxp.reshape(NCHUNK, nff, TQ, HL)

        def part(s):
            return lax.dynamic_index_in_dim(parts, lax.rem(y_me + s, nff), axis=1, keepdims=False)

        got = [shift(part(s), s) for s in range(1, nff)]
        dw_up, dw_down = weight_grads(x_loc, d_loc, m_all, du_all)
        acc = part(0).astype(F32)
        for v in got:
            acc = acc + v.astype(F32)
        mine = (ALPHA * drq + acc).astype(BF16)
        out = jnp.zeros((NCHUNK, nff, TQ, HL), BF16)
        out = lax.dynamic_update_index_in_dim(out, mine, y_me, axis=1)
        for s in range(1, nff):
            out = lax.dynamic_update_index_in_dim(out, shift(mine, s), lax.rem(y_me + nff - s, nff), axis=1)
        dx_loc = out.reshape(T, HL)
        return (y_loc, dx_loc, dw_up, dw_down, db1.reshape(-1), small[0], small[1], small[2])

    return jax.shard_map(device_step, mesh=mesh, in_specs=in_specs, out_specs=out_specs, check_vma=False)
```

time: 437 us -> 197 us (0.45)
  waiting for transfers between devices: 197 us -> 5.37 us
  Pallas kernels: 0 us -> 173 us
  matrix products: 70.7 us -> 0 us
  local copies, waits for them, and re-layouts: 64.6 us -> 5.51 us
  other arithmetic: 58.9 us -> 1 us
  blocking collectives: 25 us -> 0 us
  between operations: 14.3 us -> 0.74 us
  starting transfers between devices: 0.64 us -> 8.96 us
    psum x4 -> x0, waiting for transfers between devices: 196 us -> none  [the longest x1 101 us: device_step(): u_summed = lax.psum(u_part.astype(jnp.bfloat16), 'hd')]
    pallas_call x0 -> x3, Pallas kernels: none -> 173 us  [the longest x1 147 us: comm_call(): pl.pallas_call(functools.partial(mlp_kernel, (nff, nhd, T, HL, UH, FB)),...]
    dot_general x6 -> x0, matrix products: 70.7 us -> none  [the longest x1 19.5 us: device_step(): jnp.einsum('tbkc,hbkc->th', du_b, w_up4, preferred_element_type=jnp.float32)]
    convert_element_type x4 -> x0, other arithmetic: 30.9 us -> none  [the longest x1 11.6 us: device_step(): val_half = u_act[:, :, 0, :].astype(jnp.float32)]
    psum x2 -> x0, blocking collectives: 25 us -> none  [the longest x1 12.5 us: device_step(): lax.psum(jnp.stack([jnp.sum(residual, axis=1), jnp.sum(residual * residua...]
    convert_element_type x3 -> x0, local copies, waits for them, and re-layouts: 24.4 us -> none  [the longest x1 9.02 us: device_step(): val_half = u_act[:, :, 0, :].astype(jnp.float32)]
    reshape x2 -> x1, local copies, waits for them, and re-layouts: 20.7 us -> 1.39 us  [comm_call(): b1.reshape(nhd, 2 * UH)]
    unnamed x17 -> x10, local copies, waits for them, and re-layouts: 19.4 us -> 1.52 us
  transfers between devices with their start and end apart: 4 -> 6, of which waited for: 3 -> 2; matrix products, arithmetic and copies ran while one was open for 12% -> 1% of each run, Pallas kernels for 0% -> 13%
where the time goes in v1:
time: 197 us; the launch traced here: 194 us
  Pallas kernels  173 us (88%)
  starting transfers between devices  8.96 us (5%)
  local copies, waits for them, and re-layouts  5.51 us (3%)
  waiting for transfers between devices  5.37 us (3%)
    pallas_call x1, Pallas kernels, comm_call(): pl.pallas_call(functools.partial(mlp_kernel, (nff, nhd, T, HL, UH, FB)),...  147 us
    pallas_call x1, Pallas kernels, weight_grads(): pl.pallas_call(dw1_kernel, grid=(n1,), out_shape=jax.ShapeDtypeStruct((HL...  16.7 us
    pallas_call x1, Pallas kernels, weight_grads(): pl.pallas_call(dw2_kernel, grid=(n2,), out_shape=jax.ShapeDtypeStruct((n2...  8.97 us
    ppermute x6, starting transfers between devices, shift(): return lax.ppermute(v, 'ff', [(i, (i + s) % nff) for i in range(nff)])  8.96 us
    ppermute x6, waiting for transfers between devices, shift(): return lax.ppermute(v, 'ff', [(i, (i + s) % nff) for i in range(nff)])  5.37 us
  transfers between devices with their start and end apart: 6, of which 2 were waited for; matrix products, arithmetic and copies ran while one was open for 1% of the time, Pallas kernels for 13%

profile of v1, /device:TPU:96, one launch (start us, length us, event | category | flops | bytes accessed | tf_op | source)
XLA Modules:
  0.0 194.4 jit_solution(13681068251798511885)
XLA Ops:
  0.7 1.4 reshape.42.b1_ref
  2.0 147.1 %mlp_comm.1 = (bf16[512,512]{1,0:T(8,128)(2,1)}, bf16[512,512]{1,0:T(8,128)(2,1)}, bf16[8,512,512]{2,1,0:T(8,128)(2,1)}, bf16[16,512,512]{2,1,0:T(8,128)(2,1)}, ...) custom-call(bf16[512,512]{1,0:T(8,128)(2,1)} %x_ref.1, ...), custom_call_target="tpu_custom_call" | custom-call | tf_op jit(solution)/shard_map/mlp_comm/pallas_call | solution.py:456
  149.2 1.1 dynamic-slice_bitcast_fusion.2
  150.2 1.9 collective-permute-start.2
  152.1 0.5 collective-permute-start.1
  152.6 0.9 collective-permute-start
  153.5 0.0 copy-start.2
  153.5 16.7 %dw1.1 = f32[512,8192]{1,0:T(8,128)} custom-call(bf16[512,512]{1,0:T(8,128)(2,1)} %x_ref.1, bf16[16,512,512]{2,1,0:T(8,128)(2,1)} %get-tuple-element.19.du_ref), custom_call_target="tpu_custom_call" | custom-call | flops 4294967296 | bytes 25165824 | tf_op jit(solution)/shard_map/dw1/pallas_call | solution.py:487
  170.2 0.0 copy-start
  170.2 1.4 fusion.5
  171.6 0.0 collective-permute-done.2
  171.6 0.0 collective-permute-done.1
  171.6 0.0 collective-permute-done
  171.7 0.0 copy-done.2
  171.7 0.0 copy-start.3
  171.7 1.0 bitcast_dynamic-update-slice_fusion.3
  172.7 2.2 %collective-permute-start.3 = (bf16[2,64,512]{2,1,0:T(8,128)(2,1)S(1)}, bf16[2,64,512]{2,1,0:T(8,128)(2,1)S(1)}, u32[]{:S(2)}, u32[]{:S(2)}) collective-permute-start(bf16[2,64,512]{2,1,0:T(8,128)(2,1)S(1)} %get-tuple-element.25), channel_id=1, source_target_pairs={{0,8},{8,16},{16,24},{24,0},{1,9},{9,17},{17,25},{25,1},{2,10},{10... | collective-permute-start | bytes 393224 | tf_op jit(solution)/shard_map/ppermute | solution.py:505
  174.9 9.0 %dw2.1 = f32[4096,512]{1,0:T(8,128)} custom-call(bf16[8,512,512]{2,1,0:T(8,128)(2,1)} %get-tuple-element.20.m_ref, bf16[512,512]{1,0:T(8,128)(2,1)} %get-tuple-element.21.d_ref), custom_call_target="tpu_custom_call" | custom-call | flops 2147483648 | bytes 12582912 | tf_op jit(solution)/shard_map/dw2/pallas_call | solution.py:480
  183.9 1.7 collective-permute-start.4
  185.6 1.8 collective-permute-start.5
  187.4 0.0 collective-permute-done.3
  187.4 4.4 %collective-permute-done.4 = bf16[2,64,512]{2,1,0:T(8,128)(2,1)S(1)} collective-permute-done((bf16[2,64,512]{2,1,0:T(8,128)(2,1)S(1)}, bf16[2,64,512]{2,1,0:T(8,128)(2,1)S(1)}, u32[]{:S(2)}, u32[]{:S(2)}) %collective-permute-start.4) | collective-permute-done | bytes 131104 | tf_op jit(solution)/shard_map/ppermute | solution.py:505
  191.9 1.0 collective-permute-done.5
  192.8 0.0 copy-start.1
  192.9 0.0 copy-done
  192.9 0.9 copy.28
  193.7 0.0 copy-done.3
  193.7 0.6 copy.29
  194.4 0.0 copy-done.1
  (5 shorter events, 0.1 us)
Async XLA Ops:
  150.2 21.4 %collective-permute-start.2 = (bf16[2,64,512]{2,1,0:T(8,128)(2,1)S(1)}, bf16[2,64,512]{2,1,0:T(8,128)(2,1)S(1)}, u32[]{:S(2)}, u32[]{:S(2)}) collective-permute-start(bf16[2,64,512]{2,1,0:T(8,128)(2,1)S(1)} %get-tuple-element.27), channel_id=1, source_target_pairs={{0,24},{8,0},{16,8},{24,16},{1,25},{9,1},{17,9},{25,17},{2,26},{10... | collective-permute-start | bytes 393224 | tf_op jit(solution)/shard_map/ppermute | solution.py:505
  152.1 19.5 %collective-permute-start.1 = (bf16[2,64,512]{2,1,0:T(8,128)(2,1)S(1)}, bf16[2,64,512]{2,1,0:T(8,128)(2,1)S(1)}, u32[]{:S(2)}, u32[]{:S(2)}) collective-permute-start(bf16[2,64,512]{2,1,0:T(8,128)(2,1)S(1)} %get-tuple-element.28), channel_id=1, source_target_pairs={{0,16},{8,24},{16,0},{24,8},{1,17},{9,25},{17,1},{25,9},{2,18},{10... | collective-permute-start | bytes 393224 | tf_op jit(solution)/shard_map/ppermute | solution.py:505
  152.6 19.0 %collective-permute-start = (bf16[2,64,512]{2,1,0:T(8,128)(2,1)S(1)}, bf16[2,64,512]{2,1,0:T(8,128)(2,1)S(1)}, u32[]{:S(2)}, u32[]{:S(2)}) collective-permute-start(bf16[2,64,512]{2,1,0:T(8,128)(2,1)S(1)} %get-tuple-element.26), channel_id=1, source_target_pairs={{0,8},{8,16},{16,24},{24,0},{1,9},{9,17},{17,25},{25,1},{2,10},{10... | collective-permute-start | bytes 393224 | tf_op jit(solution)/shard_map/ppermute | solution.py:505
  153.5 18.2 %copy-start.2 = (f32[2,64,512]{2,1,0:T(8,128)S(1)}, f32[2,64,512]{2,1,0:T(8,128)}, u32[]{:S(2)}) copy-start(f32[2,64,512]{2,1,0:T(8,128)} %get-tuple-element.17) | copy-start | bytes 786436
  170.2 22.7 %copy-start = (bf16[512,512]{1,0:T(8,128)(2,1)S(1)}, bf16[512,512]{1,0:T(8,128)(2,1)}, u32[]{:S(2)}) copy-start(bf16[512,512]{1,0:T(8,128)(2,1)} %get-tuple-element.40) | copy-start | bytes 1572868
  171.7 22.1 %copy-start.3 = (f32[8,8,128]{2,1,0:T(8,128)S(1)}, f32[8,8,128]{2,1,0:T(8,128)}, u32[]{:S(2)}) copy-start(f32[8,8,128]{2,1,0:T(8,128)} %get-tuple-element.22) | copy-start | bytes 98308
  172.7 14.7 %collective-permute-start.3 = (bf16[2,64,512]{2,1,0:T(8,128)(2,1)S(1)}, bf16[2,64,512]{2,1,0:T(8,128)(2,1)S(1)}, u32[]{:S(2)}, u32[]{:S(2)}) collective-permute-start(bf16[2,64,512]{2,1,0:T(8,128)(2,1)S(1)} %get-tuple-element.25), channel_id=1, source_target_pairs={{0,8},{8,16},{16,24},{24,0},{1,9},{9,17},{17,25},{25,1},{2,10},{10... | collective-permute-start | bytes 393224 | tf_op jit(solution)/shard_map/ppermute | solution.py:505
  183.9 7.9 %collective-permute-start.4 = (bf16[2,64,512]{2,1,0:T(8,128)(2,1)S(1)}, bf16[2,64,512]{2,1,0:T(8,128)(2,1)S(1)}, u32[]{:S(2)}, u32[]{:S(2)}) collective-permute-start(bf16[2,64,512]{2,1,0:T(8,128)(2,1)S(1)} %get-tuple-element.25), channel_id=1, source_target_pairs={{0,16},{8,24},{16,0},{24,8},{1,17},{9,25},{17,1},{25,9},{2,18},{10... | collective-permute-start | bytes 393224 | tf_op jit(solution)/shard_map/ppermute | solution.py:505
  185.6 7.2 %collective-permute-start.5 = (bf16[2,64,512]{2,1,0:T(8,128)(2,1)S(1)}, bf16[2,64,512]{2,1,0:T(8,128)(2,1)S(1)}, u32[]{:S(2)}, u32[]{:S(2)}) collective-permute-start(bf16[2,64,512]{2,1,0:T(8,128)(2,1)S(1)} %get-tuple-element.25), channel_id=1, source_target_pairs={{0,24},{8,0},{16,8},{24,16},{1,25},{9,1},{17,9},{25,17},{2,26},{10... | collective-permute-start | bytes 393224 | tf_op jit(solution)/shard_map/ppermute | solution.py:505
  192.8 1.5 copy-start.1

commit v2 on v1

--- a/solution.py
+++ b/solution.py
@@ -32,10 +32,10 @@
 
 
 def mlp_kernel(cfg, x_hbm, w1_hbm, b1_ref, w2_hbm, b2_ref, gam_ref, bet_ref, dy_hbm,
-               y_out, d_out, m_out, du_out, dxp_out, drq_out, db1_out, small_out,
+               y_out, d_out, mt_out, du_out, dx_out, xt_out, db1_out, small_out,
                xo, xx, dyv, w1v, w1x, w2v, w2x,
                ps1, rf1, rn1, own1, ps2, rf2, rn2, own2, uo, mb, dub,
-               facc, fs, fr, rbuf, drq, st, do, dx, yv, dbuf, cs, csr, dxacc, dxs,
+               facc, fs, fr, rbuf, drq, st, do, dx, yv, dbuf, cs, csr, dxacc, dxs, dxr, dxv, mt, xt,
                s_sem, r_sem, l_sem):
     nff, nhd, T, HL, UH, FB = cfg
     nx = nhd // CORES
@@ -114,11 +114,14 @@
     lcopy("w2", w2_hbm, w2v)
     pl.semaphore_wait(bar, nhd - 1 + nff - 1)
     rsend("xx", x_hbm, xx, CO)
-    for j, off in enumerate(order):
+
+    def push_w1(j):
+        q = quarter(order[j])
         for h in range(2):
-            q = quarter(off)
             rsend(("w1x", j, h), load_half(c_ot * nx + q, h), w1x.at[2 * q + h], CO)
-    rsend("w2x", w2_hbm.at[pl.ds(c_ot * nx, nx)], w2x, CO)
+
+    for j in range(3):
+        push_w1(j)
     for q in range(nx):
         for h in range(2):
             b = c_ot * nx + q
@@ -127,14 +130,16 @@
     def rows(k):
         return pl.ds(k * TC, TC)
 
-    def rs_first(tag, k, j, ps, rf, rn):
-        if j == 0:
-            rsend((tag, "fA", k), ps.at[0, 0, rows(k)], rf.at[0, rows(k)], XP)
-            rsend((tag, "fB", k), ps.at[0, 1, rows(k)], rf.at[1, rows(k)], XM)
-        elif j == 1:
-            rsend((tag, "nB", k), ps.at[1, 1, rows(k)], rn.at[0, 1, rows(k)], XP)
-        elif j == 2:
-            rsend((tag, "nA", k), ps.at[2, 0, rows(k)], rn.at[1, 0, rows(k)], XM)
+    def rs_first(tag, k, j, ps, rf, rn, only=None):
+        for h in (0, 1) if only is None else (only,):
+            if j == 0 and h == 0:
+                rsend((tag, "fA", k), ps.at[0, 0, rows(k)], rf.at[0, rows(k)], XP)
+            elif j == 0:
+                rsend((tag, "fB", k), ps.at[0, 1, rows(k)], rf.at[1, rows(k)], XM)
+            elif j == 1 and h == 1:
+                rsend((tag, "nB", k), ps.at[1, 1, rows(k)], rn.at[0, 1, rows(k)], XP)
+            elif j == 2 and h == 0:
+                rsend((tag, "nA", k), ps.at[2, 0, rows(k)], rn.at[1, 0, rows(k)], XM)
 
     def rs_combine(tag, k, ps, rf, rn):
         for d, (nm, out, j, h, dev) in enumerate((("fA", "cA", 1, 0, XP), ("fB", "cB", 2, 1, XM))):
@@ -161,13 +166,22 @@
         rsend((tag, "fB", k), view(bp, rb), view(bp, rb), XM)
         rsend((tag, "o2", k), view(bp, rows(k)), view(bp, rows(k)), CO)
 
-    def ag_last(tag, k, view):
+    def oblock(off):
+        return c_ot * nx + quarter(off)
+
+    def ag_last(tag, k, view, use):
+        for off in (0, nx - 1, 1):
+            use(block(off))
+        for i, off in ((0, 0), (1, nx - 1), (2, 1)):
+            rwait((tag, "o%d" % i, k))
+            use(oblock(off))
         bf = block(2)
         rwait((tag, "fA", k))
         rwait((tag, "fB", k))
         rsend((tag, "o3", k), view(bf, rows(k)), view(bf, rows(k)), CO)
-        for i in range(4):
-            rwait((tag, "o%d" % i, k))
+        use(bf)
+        rwait((tag, "o3", k))
+        use(oblock(2))
 
     def m_view(b, r):
         return mb.at[b, r]
@@ -177,39 +191,45 @@
 
     def u_partial(k):
         for j, off in enumerate(order):
-            for h in range(2):
-                if k == 0:
-                    lwait(("w1", j, h))
-                    rwait(("w1x", j, h))
             b, q = block(off), quarter(off)
 
-            @pl.loop(0, 2)
-            def _(h):
+            def half(h):
                 p = dot_nn(xo[rows(k)], w1v[2 * b + h]) + dot_nn(xx[rows(k)], w1x[2 * q + h])
                 if j < 3:
                     ps1[j, h, rows(k)] = p.astype(BF16)
                 else:
                     own1[h, rows(k)] = p
 
-            if k == 0:
-                rs_first("U", k, j, ps1, rf1, rn1)
-
-    def u_send(k):
-        for j in range(3):
+            if k > 0:
+                pl.loop(0, 2)(half)
+            else:
+                for h in ((1, 0) if j == 1 else (0, 1)):
+                    lwait(("w1", j, h))
+                    rwait(("w1x", j, h))
+                    half(h)
+                    rs_first("U", k, j, ps1, rf1, rn1, h)
+                if j == 1:
+                    push_w1(3)
+                    rsend("w2x", w2_hbm.at[pl.ds(c_ot * nx, nx)], w2x, CO)
+
+    def u_send(k, js):
+        for j in js:
             rs_first("U", k, j, ps1, rf1, rn1)
 
     TS = 32
 
     def activate(k):
         rs_wait("U", k)
-        bias = b1_ref[pl.ds(b_own, 1), :]
+        bias = b1_ref[b_own]
+        nsl = UH // PAIR
 
         @pl.loop(0, TC // TS)
         def _(i):
             r = pl.ds(pl.multiple_of(k * TC + i * TS, TS), TS)
             for h in range(2):
                 u = own1[h, r] + rn1[0, h, r].astype(F32) + rn1[1, h, r].astype(F32)
-                u = (u + bias[:, h * UH:(h + 1) * UH]).astype(BF16)
+                u = jnp.concatenate([u[:, p * PAIR:(p + 1) * PAIR] + bias[h * nsl + p:h * nsl + p + 1, :] for p in range(nsl)], axis=1)
+                u = u.astype(BF16)
                 uo[h, r] = u
                 for p in range(UH // (2 * PAIR)):
                     v = u[:, 2 * p * PAIR:(2 * p + 1) * PAIR].astype(F32)
@@ -222,16 +242,14 @@
         ag_first("M", k, m_view)
 
     def f_partial(k):
-        ag_last("M", k, m_view)
-        lcopy(("mo", k), mb.at[:, rows(k)], m_out.at[:, rows(k)])
         facc[k] = jnp.zeros_like(facc[k])
         if k == 0:
             lwait("w2")
 
-        @pl.loop(0, nhd)
-        def _(b):
+        def use(b):
             facc[k] += dot_nn(mb[b, rows(k)], w2v[b])
 
+        ag_last("M", k, m_view, use)
         fs[rows(k)] = facc[k].astype(BF16)
         for s in range(1, nff):
             yy = lax.rem(y_me + s, nff)
@@ -352,20 +370,43 @@
         ag_first("V", k, du_view)
 
     def dx_partial(k):
-        ag_last("V", k, du_view)
-        lcopy(("duo", k), dub.at[:, rows(k)], du_out.at[:, rows(k)])
-        dxacc[...] = jnp.zeros_like(dxacc)
+        dxacc[k] = jnp.zeros_like(dxacc[k])
         if k == 0:
             for q in range(nx):
                 for h in range(2):
                     lwait(("w1o", q, h))
 
-        @pl.loop(0, 2 * nhd)
-        def _(i):
-            dxacc[...] += dot_nt(dub[i, rows(k)], w1v[i])
-
-        dxs[rows(k)] = dxacc[...].astype(BF16)
-        lcopy(("dxo", k), dxs.at[rows(k)], dxp_out.at[rows(k)])
+        def use(b):
+            @pl.loop(0, 2)
+            def _(h):
+                dxacc[k] += dot_nt(dub[2 * b + h, rows(k)], w1v[2 * b + h])
+
+        ag_last("V", k, du_view, use)
+        lcopy(("duo", k), dub.at[:, rows(k)], du_out.at[:, rows(k)])
+        dxs[rows(k)] = dxacc[k].astype(BF16)
+        for s in range(1, nff):
+            rsend(("xr", s, k), dxs.at[q_rows(k, lax.rem(y_me + s, nff))], dxr.at[k, s - 1], ydev(s))
+
+    def dx_sum(k):
+        for s in range(1, nff):
+            rwait(("xr", s, k))
+        v = dxacc[k, pl.ds(pl.multiple_of(y_me * TQ, TQ), TQ)]
+        for s in range(1, nff):
+            v = v + dxr[k, s - 1].astype(F32)
+        qr = q_rows(k, y_me)
+        dxv[qr] = (ALPHA * drq[k] + v).astype(BF16)
+        for s in range(1, nff):
+            rsend(("xg", s, k), dxv.at[qr], dxv.at[qr], ydev(s))
+
+    def dx_done(k):
+        for s in range(1, nff):
+            rwait(("xg", s, k))
+        lcopy(("dxo", k), dxv.at[rows(k)], dx_out.at[rows(k)])
+
+    def transpose_m(lo, hi):
+        @pl.loop(lo, hi)
+        def _(b):
+            mt[b] = mb[b].T
 
     cs[...] = jnp.zeros_like(cs)
     dbuf[b_own] = jnp.zeros_like(dbuf[b_own])
@@ -374,35 +415,45 @@
     u_partial(0)
     u_partial(1)
     rs_combine("U", 0, ps1, rf1, rn1)
-    u_send(1)
+    u_send(1, (0,))
     activate(0)
+    u_send(1, (1, 2))
+    xt[...] = xo[...].T
+    lcopy("xto", xt, xt_out)
+    ag_forward("M", 0, m_view)
     rs_combine("U", 1, ps1, rf1, rn1)
-    ag_forward("M", 0, m_view)
+    f_partial(0)
+    ln_stats(0)
     activate(1)
-    f_partial(0)
+    ln_apply(0)
     ag_forward("M", 1, m_view)
-    ln_stats(0)
-    ln_apply(0)
+    d_forward(0)
+    dm_partial(0)
     f_partial(1)
-    d_forward(0)
+    rs_combine("G", 0, ps2, rf2, rn2)
     ln_stats(1)
-    dm_partial(0)
+    du_make(0)
     ln_apply(1)
-    rs_combine("G", 0, ps2, rf2, rn2)
     for s in range(1, nff):
         rsend(("cs", s), cs, csr.at[s - 1], ydev(s))
     d_forward(1)
-    du_make(0)
     dm_partial(1)
+    rs_combine("G", 1, ps2, rf2, rn2)
     ag_forward("V", 0, du_view)
-    rs_combine("G", 1, ps2, rf2, rn2)
+    transpose_m(0, nhd // 2)
+    early = list(sent)
+    sent.clear()
     du_make(1)
     for s in range(1, nhd):
         rsend(("db", s), dbuf.at[b_own], dbuf.at[b_own], hdev(s))
     dx_partial(0)
+    transpose_m(nhd // 2, nhd)
+    lcopy("mto", mt, mt_out)
+    dx_sum(0)
+    for cp in early:
+        cp.wait_send()
     ag_forward("V", 1, du_view)
     lcopy("do", do, d_out)
-    lcopy("dro", drq, drq_out)
     for k in range(NCHUNK):
         for s in range(1, nff):
             rwait(("y", s, k))
@@ -417,11 +468,14 @@
     for s in range(1, nhd):
         rwait(("db", s))
     db1_out[...] = dbuf[...]
+    dx_done(0)
     dx_partial(1)
-    for nm in ("do", "dro", "yo"):
+    dx_sum(1)
+    dx_done(1)
+    for nm in ("do", "xto", "yo", "mto"):
         lwait(nm)
     for k in range(NCHUNK):
-        for nm in ("mo", "duo", "dxo"):
+        for nm in ("duo", "dxo"):
             lwait((nm, k))
     for cp in sent:
         cp.wait_send()
@@ -447,7 +501,8 @@
         V((NCHUNK, TQ, HL), F32), V((NCHUNK, TQ, HL), F32), V((NCHUNK, nhd, 8, 128), F32),
         V((T, HL), BF16), V((T, HL), BF16), V((T, HL), BF16),
         V((nhd, 2 * UH // 128, 128), F32), V((8, HL), F32), V((nff - 1, 8, HL), F32),
-        V((TC, HL), F32), V((T, HL), BF16),
+        V((NCHUNK, TC, HL), F32), V((T, HL), BF16), V((NCHUNK, nff - 1, TQ, HL), BF16), V((T, HL), BF16),
+        V((nhd, FB, T), BF16), V((HL, T), BF16),
         pltpu.SemaphoreType.DMA((160,)), pltpu.SemaphoreType.DMA((160,)), pltpu.SemaphoreType.DMA((40,)),
     ]
     anyspec = pl.BlockSpec(memory_space=pl.ANY)
@@ -455,77 +510,103 @@
     S = jax.ShapeDtypeStruct
     return pl.pallas_call(
         functools.partial(mlp_kernel, (nff, nhd, T, HL, UH, FB)),
-        out_shape=[S((T, HL), BF16), S((T, HL), BF16), S((nhd, T, FB), BF16), S((2 * nhd, T, UH), BF16),
-                   S((T, HL), BF16), S((NCHUNK, TQ, HL), F32), S((nhd, 2 * UH // 128, 128), F32), S((8, HL), F32)],
+        out_shape=[S((T, HL), BF16), S((T, HL), BF16), S((nhd, FB, T), BF16), S((2 * nhd, T, UH), BF16),
+                   S((T, HL), BF16), S((HL, T), BF16), S((nhd, 2 * UH // 128, 128), F32), S((8, HL), F32)],
         in_specs=[anyspec, anyspec, vspec, anyspec, vspec, vspec, vspec, anyspec],
         out_specs=[anyspec, anyspec, anyspec, anyspec, anyspec, anyspec, vspec, vspec],
         scratch_shapes=scratch,
         compiler_params=pltpu.CompilerParams(collective_id=0, has_side_effects=True, vmem_limit_bytes=67043328),
         name="mlp_comm",
-    )(x, w1, b1.reshape(nhd, 2 * UH), w2.reshape(nhd, FB, HL), b2.reshape(1, HL), gam.reshape(1, HL), bet.reshape(1, HL), dy)
-
-
-def dw2_kernel(m_ref, d_ref, o_ref):
-    o_ref[...] = dot_tn(m_ref[0], d_ref[...])
-
-
-def dw1_kernel(x_ref, du_ref, o_ref):
-    o_ref[...] = dot_tn(x_ref[...], du_ref[0])
-
-
-def weight_grads(x, d, m, du):
-    n2, T, FB = m.shape
+    )(x, w1, b1.reshape(nhd, 2 * UH // PAIR, PAIR), w2.reshape(nhd, FB, HL), b2.reshape(1, HL), gam.reshape(1, HL), bet.reshape(1, HL), dy)
+
+
+def grads_kernel(xt_hbm, du_hbm, mt_hbm, d_hbm, y_hbm, dx_hbm, db1_ref, small_ref,
+                 dw1_hbm, dw2_hbm, y_out, dx_out, db1_out, db2_out, dg_out, db_out,
+                 xt, du, mt, d, yv, xv, o1, o2, in_sem, du_sem, mt_sem, o1_sem, o2_sem):
+    n1, n2 = du.shape[0], mt.shape[0]
+    UH, FB = du.shape[2], mt.shape[1]
+    small = [pltpu.make_async_copy(a, b, in_sem.at[i]) for i, (a, b) in enumerate(
+        ((d_hbm, d), (xt_hbm, xt), (y_hbm, yv), (dx_hbm, xv), (yv, y_out), (xv, dx_out)))]
+
+    def du_load(i):
+        return pltpu.make_async_copy(du_hbm.at[i], du.at[i], du_sem.at[i])
+
+    def mt_load(i):
+        return pltpu.make_async_copy(mt_hbm.at[i], mt.at[i], mt_sem.at[i])
+
+    def o1_store(i):
+        return pltpu.make_async_copy(o1.at[i], dw1_hbm.at[:, pl.ds(pl.multiple_of(i * UH, UH), UH)], o1_sem.at[i])
+
+    def o2_store(i):
+        return pltpu.make_async_copy(o2.at[i], dw2_hbm.at[pl.ds(pl.multiple_of(i * FB, FB), FB)], o2_sem.at[i])
+
+    small[0].start()
+    small[1].start()
+    pl.loop(0, n2)(lambda i: mt_load(i).start())
+    pl.loop(0, n1)(lambda i: du_load(i).start())
+    small[2].start()
+    small[3].start()
+    db1_out[...] = db1_ref[...]
+    db2_out[...] = small_ref[0:1, :]
+    dg_out[...] = small_ref[1:2, :]
+    db_out[...] = small_ref[2:3, :]
+    small[0].wait()
+    small[1].wait()
+
+    @pl.loop(0, n2)
+    def _(i):
+        mt_load(i).wait()
+        o2[i] = dot_nn(mt[i], d[...])
+        o2_store(i).start()
+
+    @pl.loop(0, n1)
+    def _(i):
+        du_load(i).wait()
+        o1[i] = dot_nn(xt[...], du[i])
+        o1_store(i).start()
+
+    for i in (2, 3):
+        small[i].wait()
+        small[i + 2].start()
+    pl.loop(0, n2)(lambda i: o2_store(i).wait())
+    pl.loop(0, n1)(lambda i: o1_store(i).wait())
+    for i in (4, 5):
+        small[i].wait()
+
+
+def weight_grads(xt, du, mt, d, y, dx, db1, small):
+    n2, FB, T = mt.shape
     n1, _, UH = du.shape
-    HL = x.shape[1]
-    dw2 = pl.pallas_call(
-        dw2_kernel, grid=(n2,), out_shape=jax.ShapeDtypeStruct((n2 * FB, HL), F32),
-        in_specs=[pl.BlockSpec((1, T, FB), lambda i: (i, 0, 0)), pl.BlockSpec((T, HL), lambda i: (0, 0))],
-        out_specs=pl.BlockSpec((FB, HL), lambda i: (i, 0)),
-        cost_estimate=pl.CostEstimate(flops=2 * n2 * FB * HL * T, bytes_accessed=n2 * FB * HL * 4 + n2 * FB * T * 2, transcendentals=0),
-        name="dw2",
-    )(m, d)
-    dw1 = pl.pallas_call(
-        dw1_kernel, grid=(n1,), out_shape=jax.ShapeDtypeStruct((HL, n1 * UH), F32),
-        in_specs=[pl.BlockSpec((T, HL), lambda i: (0, 0)), pl.BlockSpec((1, T, UH), lambda i: (i, 0, 0))],
-        out_specs=pl.BlockSpec((HL, UH), lambda i: (0, i)),
-        cost_estimate=pl.CostEstimate(flops=2 * n1 * UH * HL * T, bytes_accessed=n1 * UH * HL * 4 + n1 * UH * T * 2, transcendentals=0),
-        name="dw1",
-    )(x, du)
-    return dw1, dw2
+    HL = xt.shape[0]
+    S = jax.ShapeDtypeStruct
+    V = pltpu.VMEM
+    anyspec = pl.BlockSpec(memory_space=pl.ANY)
+    vspec = pl.BlockSpec(memory_space=pltpu.VMEM)
+    dma = pltpu.SemaphoreType.DMA
+    return pl.pallas_call(
+        grads_kernel,
+        out_shape=[S((HL, n1 * UH), F32), S((n2 * FB, HL), F32), S(y.shape, BF16), S(dx.shape, BF16),
+                   S(db1.shape, F32), S((1, HL), F32), S((1, HL), F32), S((1, HL), F32)],
+        in_specs=[anyspec] * 6 + [vspec] * 2,
+        out_specs=[anyspec] * 4 + [vspec] * 4,
+        scratch_shapes=[V((HL, T), BF16), V((n1, T, UH), BF16), V((n2, FB, T), BF16), V((T, HL), BF16), V((T, HL), BF16), V((T, HL), BF16),
+                        V((n1, HL, UH), F32), V((n2, FB, HL), F32), dma((6,)), dma((n1,)), dma((n2,)), dma((n1,)), dma((n2,))],
+        compiler_params=pltpu.CompilerParams(vmem_limit_bytes=67043328),
+        cost_estimate=pl.CostEstimate(flops=2 * T * HL * (n1 * UH + n2 * FB), bytes_accessed=(n1 * UH + n2 * FB) * (4 * HL + 2 * T), transcendentals=0),
+        name="weight_grads",
+    )(xt, du, mt, d, y, dx, db1, small)
 
 
 def solution(mesh):
-    nff = mesh.shape['ff']
     data_spec = P('dp', 'hd')
     hid_spec = P('hd')
     in_specs = (data_spec, P('hd', 'ff'), P('ff'), P('ff', 'hd'), hid_spec, hid_spec, hid_spec, data_spec)
     out_specs = (data_spec, data_spec, P(('dp', 'hd'), 'ff'), P(('dp', 'ff'), 'hd'), P(('dp', 'ff')), P(('dp', 'hd')), P(('dp', 'hd')), P(('dp', 'hd')))
 
-    def shift(v, s):
-        return lax.ppermute(v, 'ff', [(i, (i + s) % nff) for i in range(nff)])
-
     def device_step(x_loc, w_up, b_up, w_down, b_down, ln_gain, ln_bias, dy_loc):
-        T, HL = x_loc.shape
-        y_loc, d_loc, m_all, du_all, dxp, drq, db1, small = comm_call(
+        y_loc, d_loc, mt, du, dx_loc, xt, db1, small = comm_call(
             mesh, x_loc, w_up, b_up, w_down, b_down, ln_gain, ln_bias, dy_loc)
-        y_me = lax.axis_index('ff')
-        TQ = T // (NCHUNK * nff)
-        parts = dxp.reshape(NCHUNK, nff, TQ, HL)
-
-        def part(s):
-            return lax.dynamic_index_in_dim(parts, lax.rem(y_me + s, nff), axis=1, keepdims=False)
-
-        got = [shift(part(s), s) for s in range(1, nff)]
-        dw_up, dw_down = weight_grads(x_loc, d_loc, m_all, du_all)
-        acc = part(0).astype(F32)
-        for v in got:
-            acc = acc + v.astype(F32)
-        mine = (ALPHA * drq + acc).astype(BF16)
-        out = jnp.zeros((NCHUNK, nff, TQ, HL), BF16)
-        out = lax.dynamic_update_index_in_dim(out, mine, y_me, axis=1)
-        for s in range(1, nff):
-            out = lax.dynamic_update_index_in_dim(out, shift(mine, s), lax.rem(y_me + nff - s, nff), axis=1)
-        dx_loc = out.reshape(T, HL)
-        return (y_loc, dx_loc, dw_up, dw_down, db1.reshape(-1), small[0], small[1], small[2])
+        dw_up, dw_down, y_loc, dx_loc, db1, db2, dgain, dbias = weight_grads(xt, du, mt, d_loc, y_loc, dx_loc, db1, small)
+        return (y_loc, dx_loc, dw_up, dw_down, db1.reshape(-1), db2.reshape(-1), dgain.reshape(-1), dbias.reshape(-1))
 
     return jax.shard_map(device_step, mesh=mesh, in_specs=in_specs, out_specs=out_specs, check_vma=False)

time: 197 us -> 159 us (0.81); the launches traced: 194 us -> 159 us
  Pallas kernels: 173 us -> 158 us
  starting transfers between devices: 8.96 us -> 0 us
  local copies, waits for them, and re-layouts: 5.51 us -> 0 us
  waiting for transfers between devices: 5.37 us -> 0 us
    pallas_call x2 -> x1, Pallas kernels: 25.7 us -> 15 us  [weight_grads(): pl.pallas_call(grads_kernel, out_shape=[S((HL, n1 * UH), F32), S((n2 * FB...]
    ppermute x6 -> x0, starting transfers between devices: 8.96 us -> none  [shift(): return lax.ppermute(v, 'ff', [(i, (i + s) % nff) for i in range(nff)])]
    ppermute x6 -> x0, waiting for transfers between devices: 5.37 us -> none  [shift(): return lax.ppermute(v, 'ff', [(i, (i + s) % nff) for i in range(nff)])]
    pallas_call x1, Pallas kernels: 147 us -> 143 us  [comm_call(): pl.pallas_call(functools.partial(mlp_kernel, (nff, nhd, T, HL, UH, FB)),...]
  transfers between devices with their start and end apart: 6 -> 0, of which waited for: 2 -> 0; matrix products, arithmetic and copies ran while one was open for 1% -> 0% of each run, Pallas kernels for 13% -> 0%
where the time goes in v2:
time: 159 us
  Pallas kernels  158 us (99%)
    pallas_call x1, Pallas kernels, comm_call(): pl.pallas_call(functools.partial(mlp_kernel, (nff, nhd, T, HL, UH, FB)),...  143 us
    pallas_call x1, Pallas kernels, weight_grads(): pl.pallas_call(grads_kernel, out_shape=[S((HL, n1 * UH), F32), S((n2 * FB...  15 us

profile of v2, /device:TPU:96, one launch (start us, length us, event | category | flops | bytes accessed | tf_op | source)
XLA Modules:
  0.0 158.5 jit_solution(7611133757195897476)
XLA Ops:
  0.6 142.7 %mlp_comm.1 = (bf16[512,512]{1,0:T(8,128)(2,1)}, bf16[512,512]{1,0:T(8,128)(2,1)}, bf16[8,512,512]{2,1,0:T(8,128)(2,1)}, bf16[16,512,512]{2,1,0:T(8,128)(2,1)}, ...) custom-call(bf16[512,512]{1,0:T(8,128)(2,1)} %x_hbm.1, ...), custom_call_target="tpu_custom_call" | custom-call | tf_op jit(solution)/shard_map/mlp_comm/pallas_call | solution.py:511
  143.4 15.0 %weight_grads.1 = (f32[512,8192]{1,0:T(8,128)}, f32[4096,512]{1,0:T(8,128)}, bf16[512,512]{1,0:T(8,128)(2,1)}, bf16[512,512]{1,0:T(8,128)(2,1)}, f32[8,8,128]{2,...) custom-call(bf16[512,512]{1,0:T(8,128)(2,1)} %get-tuple-element.24.xt_hbm, ...), custom_call_target="tpu_custom_call" | custom-call | flops 6442450944 | bytes 37748736 | tf_op jit(solution)/shard_map/weight_grads/pallas_call | solution.py:586
